TPU v7x, 32 devices: a whole 2x2x4 slice. The times are simulated.
32 devices in a mesh: slab: 8 (over z, x), rhs: 4 (over y, core).
Axes of the slice: x: 2, y: 2, z: 4, core: 2. Of those that a mesh axis runs over, the one named last changes fastest.
Arguments:
- targets: float32 [8, 128, 256], P('rhs', 'slab'), may hold values from -60 to 60
- counts: int32 [128], P('slab'), may hold values from 1 to 256, 20480 in all
- cell_rows: int32 [128, 256], P('slab'), may hold values from 0 to 255
- cell_cols: int32 [128, 256], P('slab'), may hold values from 0 to 127
- fractions: float32 [2, 128, 256], P(None, 'slab'), may hold values from 0 to 1
- spectrum: float32 [2048, 2048], P(None, ('slab', 'rhs')), may hold values from 0.25 to 4, as said below
- noise_var: float32 [1], replicated, may hold values from 0.1 to 1
Outputs:
- solution: float32 [8, 128, 256], P('rhs', 'slab')
- residual: float32 [8, 128, 256], P('rhs', 'slab')
Inputs may be any that keep to these rules, and one draw needn't show every extreme that they name: Each tile has 256 slots; tile t holds points in its first counts[t] slots, and the other slots are empty: their entries are ignored and their outputs are zero. Even in frequency: spectrum[a, b] = spectrum[(2048 - a) % 2048, (2048 - b) % 2048].
All inputs are finite; a program needn't handle non-finite values. No bound on the sum of `counts` on one device may be relied on, other than what follows from the above.
Results may differ from a plain program's by a relative error of at most 0.0002.
Values sent between devices are 32-bit elements; how exact they have to be, the bound alone decides.
A program may use at most 128 MiB of HBM per device.

v0:
```python
import math

import jax
import jax.numpy as jnp
from jax import lax
from jax.sharding import PartitionSpec as P

G = 2048
TC = 128
ITERS = 2


def passed_along(value, axis, steps):
    count = lax.axis_size(axis)
    pairs = [(source, (source + steps) % count) for source in range(count)]
    return lax.ppermute(value, axis, pairs)


def extended_2(cells, sides, width):
    for axis, dim in sides:
        count = lax.axis_size(axis)
        head = lax.slice_in_dim(cells, 0, width, axis=dim)
        tail = lax.slice_in_dim(cells, cells.shape[dim] - width, cells.shape[dim], axis=dim)
        cells = jnp.concatenate(
            [
                lax.ppermute(tail, axis, [(i, (i + 1) % count) for i in range(count)]),
                cells,
                lax.ppermute(head, axis, [((i + 1) % count, i) for i in range(count)]),
            ],
            axis=dim,
        )
    return cells


def cubic_weights(fraction):
    return (
        ((-0.5 * fraction + 1.0) * fraction - 0.5) * fraction,
        (1.5 * fraction - 2.5) * fraction * fraction + 1.0,
        ((-1.5 * fraction + 2.0) * fraction + 0.5) * fraction,
        (0.5 * fraction - 0.5) * fraction * fraction,
    )


def spread_table(cell_index, fraction, extent):
    weights = cubic_weights(fraction)
    position = lax.broadcasted_iota(jnp.int32, (1, extent, 1), 1)
    weight_table = jnp.zeros((cell_index.shape[0], extent, cell_index.shape[1]), jnp.float32)
    for offset in range(4):
        hit = (position == cell_index[:, None, :] + offset).astype(jnp.float32)
        weight_table = weight_table + weights[offset][:, None, :] * hit
    return weight_table


def small_factor(length):
    for factor in (16, 8, 4, 2):
        return factor
    first_len = 1
    for factor in range(1, math.isqrt(length) + 1):
        if length % factor == 0:
            first_len = factor
    return first_len


def phase_table(row_count, col_count, length, sign):
    left = lax.broadcasted_iota(jnp.int32, (row_count, col_count), 0)
    right = lax.broadcasted_iota(jnp.int32, (row_count, col_count), 1)
    angle = (left * right % length).astype(jnp.float32) * (2.0 * math.pi / length)
    return (jnp.cos(angle), sign * jnp.sin(angle))


def direct_dft(real_in, imag_in, sign):
    length = real_in.shape[1]
    cos_t, sin_t = phase_table(length, length, length, sign)
    out_real = jnp.einsum("kn,anb->akb", cos_t, real_in, precision=lax.Precision.HIGHEST)
    out_imag = jnp.einsum("kn,anb->akb", sin_t, real_in, precision=lax.Precision.HIGHEST)
    out_real = out_real - jnp.einsum("kn,anb->akb", sin_t, imag_in, precision=lax.Precision.HIGHEST)
    out_imag = out_imag + jnp.einsum("kn,anb->akb", cos_t, imag_in, precision=lax.Precision.HIGHEST)
    return (out_real, out_imag)


def contract_first(table, values):
    return jnp.einsum("kn,anmb->akmb", table, values, precision=lax.Precision.HIGHEST)


def sectioned_dft(real_in, imag_in, sign):
    lead_size, length, tail_size = real_in.shape
    first_len = small_factor(length)
    if length <= 128 or first_len == 1:
        return direct_dft(real_in, imag_in, sign)
    second_len = length // first_len
    split_shape = (lead_size, first_len, second_len, tail_size)
    cos_one, sin_one = phase_table(first_len, first_len, first_len, sign)
    real_split = real_in.reshape(split_shape)
    section_real = contract_first(cos_one, real_split)
    section_imag = contract_first(sin_one, real_split)
    imag_split = imag_in.reshape(split_shape)
    section_real = section_real - contract_first(sin_one, imag_split)
    section_imag = section_imag + contract_first(cos_one, imag_split)
    twist_cos, twist_sin = phase_table(first_len, second_len, length, sign)
    twist_cos = twist_cos[None, :, :, None]
    twist_sin = twist_sin[None, :, :, None]
    mixed_real = section_real * twist_cos - section_imag * twist_sin
    mixed_imag = section_real * twist_sin + section_imag * twist_cos
    inner_shape = (lead_size * first_len, second_len, tail_size)
    inner_real, inner_imag = sectioned_dft(
        mixed_real.reshape(inner_shape), mixed_imag.reshape(inner_shape), sign
    )
    out_real = (
        inner_real.reshape(split_shape).transpose(0, 2, 1, 3).reshape(lead_size, length, tail_size)
    )
    out_imag = (
        inner_imag.reshape(split_shape).transpose(0, 2, 1, 3).reshape(lead_size, length, tail_size)
    )
    return (out_real, out_imag)


def transform(real_part, imag_part, axis, sign):
    full_shape = real_part.shape
    length = full_shape[axis]
    if axis == len(full_shape) - 1:
        moved_real = real_part.reshape(-1, length).T.reshape(1, length, -1)
        moved_imag = imag_part.reshape(-1, length).T.reshape(1, length, -1)
        out_real, out_imag = sectioned_dft(moved_real, moved_imag, sign)
        if sign > 0:
            out_real = out_real / length
            out_imag = out_imag / length
        out_real = out_real.reshape(length, -1).T.reshape(full_shape)
        out_imag = out_imag.reshape(length, -1).T.reshape(full_shape)
        return (out_real, out_imag)
    out_real, out_imag = sectioned_dft(real_part, imag_part, sign)
    if sign > 0:
        out_real = out_real / length
        out_imag = out_imag / length
    return (out_real, out_imag)


def spread(vector, row_table, col_table, rows_dev):
    weighted = row_table[None] * vector[:, :, None, :]
    pieces = jnp.einsum("kjap,jbp->kajb", weighted, col_table, precision=lax.Precision.HIGHEST)
    batch_rhs, ext_rows, tile_count, ext_cols = pieces.shape
    main_part = pieces[..., :TC].reshape(batch_rhs, ext_rows, tile_count * TC)
    tail_part = jnp.pad(pieces[..., TC:], ((0, 0), (0, 0), (0, 0), (0, TC - 3)))
    tail_part = tail_part.reshape(batch_rhs, ext_rows, tile_count * TC)
    summed = jnp.roll(main_part, -1, axis=2) + jnp.roll(tail_part, TC - 1, axis=2)
    upper_rim = summed[:, 0:1]
    lower_rim = summed[:, rows_dev + 1 :]
    from_above = passed_along(lower_rim, "slab", 1)
    from_below = passed_along(upper_rim, "slab", -1)
    field = summed[:, 1 : rows_dev + 1]
    field = field.at[:, 0:2].add(from_above)
    field = field.at[:, rows_dev - 1 :].add(from_below)
    return field


def interpolate(field, row_table, col_table):
    padded = extended_2(field, (("slab", 1),), 2)
    rows_ext = padded[:, 1:]
    batch_rhs, ext_rows, width_all = rows_ext.shape
    tile_count = width_all // TC
    wrapped = jnp.concatenate([rows_ext[..., -1:], rows_ext, rows_ext[..., :2]], axis=2)
    main_part = wrapped[..., :width_all].reshape(batch_rhs, ext_rows, tile_count, TC)
    tail_part = jnp.pad(wrapped[..., TC:], ((0, 0), (0, 0), (0, TC - 3)))
    tail_part = tail_part.reshape(batch_rhs, ext_rows, tile_count, TC)[..., :3]
    extended = jnp.concatenate([main_part, tail_part], axis=3)
    blended = jnp.einsum("kajb,jbp->kjap", extended, col_table, precision=lax.Precision.HIGHEST)
    return jnp.sum(row_table[None] * blended, axis=2)


def smooth(field, spectrum_block):
    first_real, first_imag = transform(field[0::2], field[1::2], 2, -1.0)
    part_real, part_imag = transform(
        lax.all_to_all(first_real, "slab", split_axis=2, concat_axis=1, tiled=True),
        lax.all_to_all(first_imag, "slab", split_axis=2, concat_axis=1, tiled=True),
        1,
        -1.0,
    )
    part_real, part_imag = transform(part_real * spectrum_block, part_imag * spectrum_block, 1, 1.0)
    back_real = lax.all_to_all(part_real, "slab", split_axis=1, concat_axis=2, tiled=True)
    back_imag = lax.all_to_all(part_imag, "slab", split_axis=1, concat_axis=2, tiled=True)
    last_real, last_imag = transform(back_real, back_imag, 2, 1.0)
    return jnp.stack([last_real, last_imag], axis=1).reshape(field.shape)


def squares(residual):
    return lax.psum(jnp.sum(residual * residual, axis=(1, 2)), "slab")


def per_device(targets, counts, cell_rows, cell_cols, fractions, spectrum, noise_var):
    tile_count = cell_rows.shape[0]
    capacity = cell_rows.shape[1]
    rows_dev = G // lax.axis_size("slab")
    slot_index = lax.broadcasted_iota(jnp.int32, (tile_count, capacity), 1)
    live = (slot_index < counts[:, None]).astype(jnp.float32)
    row_table = spread_table(cell_rows, fractions[0], rows_dev + 3)
    col_table = spread_table(cell_cols, fractions[1], TC + 3)
    spectrum_block = lax.all_gather(spectrum, "rhs", axis=1, tiled=True)
    residual = live[None] * targets
    solution = jnp.zeros(residual.shape, jnp.float32)
    direction = residual
    norm_now = squares(residual)
    for repeat in range(ITERS):
        field = spread(direction, row_table, col_table, rows_dev)
        smoothed = smooth(field, spectrum_block)
        image = live[None] * interpolate(smoothed, row_table, col_table) + noise_var[0] * direction
        product = lax.psum(jnp.sum(direction * image, axis=(1, 2)), "slab")
        alpha = (norm_now / product)[:, None, None]
        solution = solution + alpha * direction
        residual = residual - alpha * image
        if repeat + 1 < ITERS:
            norm_next = squares(residual)
            direction = residual + (norm_next / norm_now)[:, None, None] * direction
            norm_now = norm_next
    return (solution, residual)


def solution(mesh):
    placed = (
        P("rhs", "slab", None),
        P("slab"),
        P("slab", None),
        P("slab", None),
        P(None, "slab", None),
        P(None, ("slab", "rhs")),
        P(),
    )
    return jax.shard_map(
        per_device,
        mesh=mesh,
        in_specs=placed,
        out_specs=(P("rhs", "slab", None), P("rhs", "slab", None)),
        check_vma=False,
    )
```

profile of v0, /device:TPU:0, one launch (start us, length us, event | category | flops | bytes accessed | tf_op | source)
XLA Modules:
  0.0 1012.2 jit_solution(3737533770023995895)
XLA Ops:
  16.8 11.2 %fusion.19 = f32[2,259,16,131]{1,3,0,2:T(8,128)S(1)} fusion(f32[2,16,256]{2,0,1:T(2,128)S(1)} %copy_multiply_fusion, f32[16,259,256]{2,1,0:T(8,128)S(1)} %select_add_fusion, f32[16,256]{1,0:T(8,128)S(1)} %get-tuple-element.98, s32[16,256]{1,0:T(8,128)S(1)} %get-tuple-element.103, f32[16,256]{1,0:T(8,128)S(1)} %get-tuple-element.99, ...), kind=kOutput, calls=%fused_computation.45 | convolution fusion | flops 3343380480 | bytes 8750208 | tf_op jit(solution)/shard_map/kjap,jbp->kajb/dot_general | solution.py:139
  121.3 10.2 %copy.295 = f32[1,256,2048]{1,0,2:T(1,128)} copy(f32[1,256,2048]{1,2,0:T(8,128)S(1)} %bitcast.742) | data formatting | bytes 4194304 | tf_op jit(solution)/shard_map/reshape | solution.py:128
  146.1 10.4 %copy.289 = f32[1,256,2048]{1,0,2:T(1,128)} copy(f32[1,256,2048]{1,2,0:T(8,128)S(1)} %bitcast.743) | data formatting | bytes 4194304 | tf_op jit(solution)/shard_map/reshape | solution.py:127
  156.4 26.5 %all-to-all-done.1 = f32[1,256,2048]{1,0,2:T(1,128)} async-done(((f32[1,256,2048]{1,0,2:T(1,128)}), f32[1,256,2048]{1,0,2:T(1,128)}, u32[]{:S(2)}, u32[]{:S(2)}) %all-to-all-start.1) | async-done | bytes 2097184 | tf_op jit(solution)/shard_map/all_to_all | solution.py:173
  206.2 28.8 %all-to-all-done = f32[1,256,2048]{1,0,2:T(1,128)} async-done(((f32[1,256,2048]{1,0,2:T(1,128)}), f32[1,256,2048]{1,0,2:T(1,128)}, u32[]{:S(2)}, u32[]{:S(2)}) %all-to-all-start) | async-done | bytes 2097184 | tf_op jit(solution)/shard_map/all_to_all | solution.py:172
  289.7 10.0 copy.321
  314.0 10.0 copy.315
  324.0 28.0 %all-to-all-done.3 = f32[1,2048,256]{2,0,1:T(1,128)} async-done(((f32[1,2048,256]{2,0,1:T(1,128)}), f32[1,2048,256]{2,0,1:T(1,128)}, u32[]{:S(2)}, u32[]{:S(2)}) %all-to-all-start.3) | async-done | bytes 2097184 | tf_op jit(solution)/shard_map/all_to_all | solution.py:179
  373.5 31.1 %all-to-all-done.2 = f32[1,2048,256]{2,0,1:T(1,128)} async-done(((f32[1,2048,256]{2,0,1:T(1,128)}), f32[1,2048,256]{2,0,1:T(1,128)}, u32[]{:S(2)}, u32[]{:S(2)}) %all-to-all-start.2) | async-done | bytes 2097184 | tf_op jit(solution)/shard_map/all_to_all | solution.py:178
  467.2 19.8 %fusion.1 = f32[2,16,256]{2,0,1:T(2,128)S(1)} fusion(f32[16,259,256]{2,1,0:T(8,128)} %copy-done.31, f32[16,256]{1,0:T(8,128)S(1)} %get-tuple-element.98, s32[16,256]{1,0:T(8,128)S(1)} %get-tuple-element.103, f32[16,256]{1,0:T(8,128)S(1)} %get-tuple-element.99, s32[16,256]{1,0:T(8,128)S(1)} %get-tuple-element.104, f32[16,256]{1,0:T(8,128)S(1)} %get-tuple-element.100, ...), kind=kOutput, calls=%fused_computation.3 | convolution fusion | flops 3346579712 | bytes 8750208 | tf_op jit(solution)/shard_map/kajb,jbp->kjap/dot_general | solution.py:165
  487.2 21.0 %all-reduce.4 = (f32[2]{0:T(128)S(1)}, f32[2]{0:T(128)S(1)}) all-reduce(f32[2]{0:T(128)S(1)} %get-tuple-element.55, f32[2]{0:T(128)S(1)} %get-tuple-element.54), channel_id=1, replica_groups=mesh['slab'=8,'rhs'=4] {'slab'}, use_global_device_ids=true, to_apply=%region_1.0 | all-reduce | flops 4 | bytes 32 | tf_op jit(solution)/shard_map/psum | solution.py:185
  508.4 17.5 %psum.30 = f32[2]{0:T(128)S(1)} all-reduce(f32[2]{0:T(128)S(1)} %get-tuple-element.58), channel_id=1, replica_groups=mesh['slab'=8,'rhs'=4] {'slab'}, use_global_device_ids=true, to_apply=%region_6.7 | all-reduce | flops 2 | bytes 16 | tf_op jit(solution)/shard_map/psum | solution.py:185
  526.1 13.2 %fusion.22 = f32[2,259,16,131]{1,3,0,2:T(8,128)S(1)} fusion(f32[2,16,256]{2,0,1:T(2,128)S(1)} %multiply_add_fusion.2, f32[16,259,256]{2,1,0:T(8,128)} %copy-done.31, f32[16,256]{1,0:T(8,128)S(1)} %get-tuple-element.98, s32[16,256]{1,0:T(8,128)S(1)} %get-tuple-element.103, f32[16,256]{1,0:T(8,128)S(1)} %get-tuple-element.99, ...), kind=kOutput, calls=%fused_computation.46 | convolution fusion | flops 3343380480 | bytes 8750208 | tf_op jit(solution)/shard_map/kjap,jbp->kajb/dot_general | solution.py:139
  631.5 10.0 copy.357
  655.5 10.0 copy.351
  665.5 17.7 %all-to-all-done.5 = f32[1,256,2048]{1,0,2:T(1,128)} async-done(((f32[1,256,2048]{1,0,2:T(1,128)}), f32[1,256,2048]{1,0,2:T(1,128)}, u32[]{:S(2)}, u32[]{:S(2)}) %all-to-all-start.5) | async-done | bytes 2097184 | tf_op jit(solution)/shard_map/all_to_all | solution.py:173
  704.4 27.2 %all-to-all-done.4 = f32[1,256,2048]{1,0,2:T(1,128)} async-done(((f32[1,256,2048]{1,0,2:T(1,128)}), f32[1,256,2048]{1,0,2:T(1,128)}, u32[]{:S(2)}, u32[]{:S(2)}) %all-to-all-start.4) | async-done | bytes 2097184 | tf_op jit(solution)/shard_map/all_to_all | solution.py:172
  786.4 10.0 copy.383
  810.5 10.0 copy.377
  820.5 27.7 %all-to-all-done.7 = f32[1,2048,256]{2,0,1:T(1,128)} async-done(((f32[1,2048,256]{2,0,1:T(1,128)}), f32[1,2048,256]{2,0,1:T(1,128)}, u32[]{:S(2)}, u32[]{:S(2)}) %all-to-all-start.7) | async-done | bytes 2097184 | tf_op jit(solution)/shard_map/all_to_all | solution.py:179
  866.7 33.9 %all-to-all-done.6 = f32[1,2048,256]{2,0,1:T(1,128)} async-done(((f32[1,2048,256]{2,0,1:T(1,128)}), f32[1,2048,256]{2,0,1:T(1,128)}, u32[]{:S(2)}, u32[]{:S(2)}) %all-to-all-start.6) | async-done | bytes 2097184 | tf_op jit(solution)/shard_map/all_to_all | solution.py:178
  953.1 8.6 pad_maximum_fusion.2
  961.8 19.8 %fusion = f32[2,16,256]{2,0,1:T(2,128)S(1)} fusion(f32[16,259,256]{2,1,0:T(8,128)} %copy-done.31, f32[16,256]{1,0:T(8,128)S(1)} %get-tuple-element.98, s32[16,256]{1,0:T(8,128)S(1)} %get-tuple-element.103, f32[16,256]{1,0:T(8,128)S(1)} %get-tuple-element.99, s32[16,256]{1,0:T(8,128)S(1)} %get-tuple-element.104, f32[16,256]{1,0:T(8,128)S(1)} %get-tuple-element.100, ...), kind=kOutput, calls=%fused_computation.1 | convolution fusion | flops 3346579712 | bytes 8750208 | tf_op jit(solution)/shard_map/kajb,jbp->kjap/dot_general | solution.py:165
  981.7 21.8 %psum.31 = f32[2]{0:T(128)S(1)} all-reduce(f32[2]{0:T(128)S(1)} %multiply_reduce_fusion), channel_id=1, replica_groups=mesh['slab'=8,'rhs'=4] {'slab'}, use_global_device_ids=true, to_apply=%region_9.10 | all-reduce | flops 2 | bytes 16 | tf_op jit(solution)/shard_map/psum | solution.py:205
  (311 shorter events, 561.3 us)
Async XLA Ops:
  66.4 13.9 %collective-permute-start.1 = (f32[2,1,2048]{2,1,0:T(1,128)S(1)}, f32[2,1,2048]{2,1,0:T(1,128)S(1)}, u32[]{:S(2)}, u32[]{:S(2)}) collective-permute-start(f32[2,1,2048]{2,1,0:T(1,128)S(1)} %maximum_add_fusion.5), channel_id=1, source_target_pairs={{0,28},{4,0},{8,4},{12,8},{16,12},{20,16},{24,20},{28,24},{1,29},{... | collective-permute-start | bytes 49160 | tf_op jit(solution)/shard_map/ppermute | solution.py:16
  73.5 6.7 collective-permute-start
  131.5 51.5 %all-to-all-start.1 = ((f32[1,256,2048]{1,0,2:T(1,128)}), f32[1,256,2048]{1,0,2:T(1,128)}, u32[]{:S(2)}, u32[]{:S(2)}) async-start(f32[1,256,2048]{1,0,2:T(1,128)} %copy.295), calls=%async_computation.1 | async-start | bytes 4194304 | tf_op jit(solution)/shard_map/all_to_all | solution.py:173
  135.8 51.7 %all-gather.2.cloned.1.call-start = ((), (), s32[]{:S(2)}) async-start(), calls=%async_computation.8 | async-start | bytes 2621440 | tf_op jit(solution)/shard_map/all_gather | solution.py:196
  182.9 52.2 %all-to-all-start = ((f32[1,256,2048]{1,0,2:T(1,128)}), f32[1,256,2048]{1,0,2:T(1,128)}, u32[]{:S(2)}, u32[]{:S(2)}) async-start(f32[1,256,2048]{1,0,2:T(1,128)} %copy.289), calls=%async_computation | async-start | bytes 4194304 | tf_op jit(solution)/shard_map/all_to_all | solution.py:172
  299.7 52.4 %all-to-all-start.3 = ((f32[1,2048,256]{2,0,1:T(1,128)}), f32[1,2048,256]{2,0,1:T(1,128)}, u32[]{:S(2)}, u32[]{:S(2)}) async-start(f32[1,2048,256]{2,0,1:T(1,128)} %copy.321), calls=%async_computation.3 | async-start | bytes 4194304 | tf_op jit(solution)/shard_map/all_to_all | solution.py:179
  352.0 52.6 %all-to-all-start.2 = ((f32[1,2048,256]{2,0,1:T(1,128)}), f32[1,2048,256]{2,0,1:T(1,128)}, u32[]{:S(2)}, u32[]{:S(2)}) async-start(f32[1,2048,256]{2,0,1:T(1,128)} %copy.315), calls=%async_computation.2 | async-start | bytes 4194304 | tf_op jit(solution)/shard_map/all_to_all | solution.py:178
  442.8 7.6 collective-permute-start.2
  446.4 6.0 collective-permute-start.3
  508.2 31.1 %copy-start.40 = (f32[2]{0:T(128)}, f32[2]{0:T(128)S(1)}, u32[]{:S(2)}) copy-start(f32[2]{0:T(128)S(1)} %div.117) | copy-start | bytes 28
  508.4 30.9 %copy-start.37 = (f32[2,16,256]{2,0,1:T(2,128)}, f32[2,16,256]{2,0,1:T(2,128)S(1)}, u32[]{:S(2)}) copy-start(f32[2,16,256]{2,0,1:T(2,128)S(1)} %get-tuple-element.59) | copy-start | bytes 98308
  581.6 6.7 collective-permute-start.4
  583.8 4.6 collective-permute-start.5
  641.5 41.7 %all-to-all-start.5 = ((f32[1,256,2048]{1,0,2:T(1,128)}), f32[1,256,2048]{1,0,2:T(1,128)}, u32[]{:S(2)}, u32[]{:S(2)}) async-start(f32[1,256,2048]{1,0,2:T(1,128)} %copy.357), calls=%async_computation.5 | async-start | bytes 4194304 | tf_op jit(solution)/shard_map/all_to_all | solution.py:173
  683.2 48.4 %all-to-all-start.4 = ((f32[1,256,2048]{1,0,2:T(1,128)}), f32[1,256,2048]{1,0,2:T(1,128)}, u32[]{:S(2)}, u32[]{:S(2)}) async-start(f32[1,256,2048]{1,0,2:T(1,128)} %copy.351), calls=%async_computation.4 | async-start | bytes 4194304 | tf_op jit(solution)/shard_map/all_to_all | solution.py:172
  796.4 51.9 %all-to-all-start.7 = ((f32[1,2048,256]{2,0,1:T(1,128)}), f32[1,2048,256]{2,0,1:T(1,128)}, u32[]{:S(2)}, u32[]{:S(2)}) async-start(f32[1,2048,256]{2,0,1:T(1,128)} %copy.383), calls=%async_computation.7 | async-start | bytes 4194304 | tf_op jit(solution)/shard_map/all_to_all | solution.py:179
  848.2 52.4 %all-to-all-start.6 = ((f32[1,2048,256]{2,0,1:T(1,128)}), f32[1,2048,256]{2,0,1:T(1,128)}, u32[]{:S(2)}, u32[]{:S(2)}) async-start(f32[1,2048,256]{2,0,1:T(1,128)} %copy.377), calls=%async_computation.6 | async-start | bytes 4194304 | tf_op jit(solution)/shard_map/all_to_all | solution.py:178
  936.5 6.6 collective-permute-start.6
  938.6 5.2 collective-permute-start.7
  961.7 19.8 %copy-start.36 = (f32[16,256]{1,0:T(8,128)S(1)}, f32[16,256]{1,0:T(8,128)}, u32[]{:S(2)}) copy-start(f32[16,256]{1,0:T(8,128)} %copy-done.34) | copy-start | bytes 49156
  961.8 41.8 %copy-start.43 = (f32[2]{0:T(128)S(1)}, f32[2]{0:T(128)}, u32[]{:S(2)}) copy-start(f32[2]{0:T(128)} %copy-done.42) | copy-start | bytes 28
  961.8 41.8 %copy-start.33 = (f32[2,16,256]{2,1,0:T(8,128)S(1)}, f32[2,16,256]{2,1,0:T(8,128)}, u32[]{:S(2)}) copy-start(f32[2,16,256]{2,1,0:T(8,128)} %param.15) | copy-start | bytes 98308
  961.8 41.8 %copy-start.38 = (f32[2,16,256]{2,0,1:T(2,128)S(1)}, f32[2,16,256]{2,0,1:T(2,128)}, u32[]{:S(2)}) copy-start(f32[2,16,256]{2,0,1:T(2,128)} %copy-done.37) | copy-start | bytes 98308
  961.8 41.8 %copy-start.41 = (f32[2]{0:T(128)S(1)}, f32[2]{0:T(128)}, u32[]{:S(2)}) copy-start(f32[2]{0:T(128)} %copy-done.40) | copy-start | bytes 28
  (45 other events, 244.5 us)
Sparse Core Ops, SparseCore 0:
  138.2 23.9 all-gather.1
where the time goes:
time: 1020 us; the launch traced here: 1010 us
  matrix products  327 us (32%)
  local copies, waits for them, and re-layouts  280 us (27%)
  waiting for transfers between devices  229 us (22%)
  blocking collectives  60.3 us (6%)
  starting transfers between devices  56.6 us (6%)
  other arithmetic  43.2 us (4%)
  between operations  16.6 us (2%)
    dot_general x32, matrix products, contract_first(): jnp.einsum('kn,anmb->akmb', table, values, precision=lax.Precision.HIGHEST)  146 us
    all_to_all x2, waiting for transfers between devices, smooth(): lax.all_to_all(part_real, 'slab', split_axis=1, concat_axis=2, tiled=True)  65 us
    all_to_all x2, waiting for transfers between devices, smooth(): lax.all_to_all(first_real, 'slab', split_axis=2, concat_axis=1, tiled=True)  56 us
    all_to_all x2, waiting for transfers between devices, smooth(): lax.all_to_all(part_imag, 'slab', split_axis=1, concat_axis=2, tiled=True)  55.8 us
    unnamed x116, local copies, waits for them, and re-layouts  46.6 us
    all_to_all x2, waiting for transfers between devices, smooth(): lax.all_to_all(first_imag, 'slab', split_axis=2, concat_axis=1, tiled=True)  44.2 us
    dot_general x2, matrix products, interpolate(): jnp.einsum('kajb,jbp->kjap', extended, col_table, precision=lax.Precision...  39.5 us
    psum x2, blocking collectives, squares(): return lax.psum(jnp.sum(residual * residual, axis=(1, 2)), 'slab')  38.5 us
  transfers between devices with their start and end apart: 17, of which 11 were waited for; matrix products, arithmetic and copies ran while one was open for 15% of the time, Pallas kernels for 0%

commit v1 on v0

v1 whole, which is shorter than its diff:
```python
import functools
import math

import jax
import jax.numpy as jnp
import numpy as np
from jax import lax
from jax.experimental import pallas as pl
from jax.experimental.pallas import tpu as pltpu
from jax.sharding import PartitionSpec as P

G = 2048
TC = 128
ITERS = 2
RADIX = 8
LONG = G // RADIX
RIM = 8
PARTS = 2
F32 = jnp.float32
BF16 = jnp.bfloat16


def cubic_weights(fraction):
    return (
        ((-0.5 * fraction + 1.0) * fraction - 0.5) * fraction,
        (1.5 * fraction - 2.5) * fraction * fraction + 1.0,
        ((-1.5 * fraction + 2.0) * fraction + 0.5) * fraction,
        (0.5 * fraction - 0.5) * fraction * fraction,
    )


def stencil_table(cell, fraction, extent):
    weights = cubic_weights(fraction)
    position = lax.broadcasted_iota(jnp.int32, (extent, cell.shape[1]), 0)
    table = jnp.zeros((extent, cell.shape[1]), F32)
    for offset in range(4):
        target = cell + (offset - 1)
        target = jnp.where(target < 0, extent - 1, target)
        table = jnp.where(position == target, weights[offset], table)
    return table


def halves(value):
    high = value.astype(BF16)
    return high, (value - high.astype(F32)).astype(BF16)


def dot_pieces(left, right, dims=(((1,), (0,)), ((), ()))):
    dot = functools.partial(lax.dot_general, dimension_numbers=dims, preferred_element_type=F32)
    return dot(left[0], right[0]) + (dot(left[0], right[1]) + dot(left[1], right[0]))


def add(a, b):
    return (a[0] + b[0], a[1] + b[1])


def sub(a, b):
    return (a[0] - b[0], a[1] - b[1])


def quarter(a, sign):
    return (-sign * a[1], sign * a[0])


def dft4(x, sign):
    p, m = add(x[0], x[2]), sub(x[0], x[2])
    q, n = add(x[1], x[3]), quarter(sub(x[1], x[3]), sign)
    return [add(p, q), add(m, n), sub(p, q), sub(m, n)]


def dft8(x, sign):
    even, odd = dft4(x[0::2], sign), dft4(x[1::2], sign)
    r = math.sqrt(0.5)
    a, c = odd[1], odd[3]
    odd = [
        odd[0],
        (r * (a[0] - sign * a[1]), r * (a[1] + sign * a[0])),
        quarter(odd[2], sign),
        (r * (-c[0] - sign * c[1]), r * (-c[1] + sign * c[0])),
    ]
    return [add(e, o) for e, o in zip(even, odd)] + [sub(e, o) for e, o in zip(even, odd)]


def spread_kernel(vec, rows, cols, frac, trig_hi, trig_lo, twist, *rest):
    outs, (field, mixed) = rest[:PARTS], rest[PARTS:]
    tiles, ext = field.shape[1], field.shape[2]
    count = outs[0].shape[0]
    width = outs[0].shape[2] // 2
    share = count // RADIX
    field[...] = jnp.zeros_like(field)

    def one_tile(t, carry):
        row_tab = stencil_table(rows[pl.ds(t, 1), :], frac[0, pl.ds(t, 1), :], ext)
        col_tab = stencil_table(cols[pl.ds(t, 1), :], frac[1, pl.ds(t, 1), :], 2 * TC)
        weighted = jnp.concatenate(
            [row_tab * vec[0, pl.ds(t, 1), :], row_tab * vec[1, pl.ds(t, 1), :]], axis=0
        )
        piece = dot_pieces(halves(weighted), halves(col_tab), (((1,), (1,)), ((), ())))
        after = lax.rem(t + 1, tiles)
        before = lax.rem(t + tiles - 1, tiles)
        low = lax.broadcasted_iota(jnp.int32, (ext, TC), 1) < TC // 2
        for k in range(2):
            block = piece[k * ext : (k + 1) * ext]
            rim = block[:, TC:]
            field[k, t] = field[k, t] + block[:, :TC]
            field[k, after] = field[k, after] + jnp.where(low, rim, 0.0)
            field[k, before] = field[k, before] + jnp.where(low, 0.0, rim)
        return carry

    lax.fori_loop(0, tiles, one_tile, 0)

    def one_strip(i, carry):
        strip = pl.ds(pl.multiple_of(i * 8, 8), 8)
        for h in range(LONG // TC):
            lanes = slice(h * TC, (h + 1) * TC)
            x = [
                (field[0, j * (LONG // TC) + h, strip, :], field[1, j * (LONG // TC) + h, strip, :])
                for j in range(RADIX)
            ]
            for d, (re, im) in enumerate(dft8(x, -1.0)):
                c = twist[d : d + 1, lanes]
                s = twist[RADIX + d : RADIX + d + 1, lanes]
                mixed[d, 0, strip, lanes] = re * c - im * s
                mixed[d, 1, strip, lanes] = re * s + im * c
        return carry

    lax.fori_loop(0, ext // 8, one_strip, 0)
    table = (trig_hi[...], trig_lo[...])
    for d in range(RADIX):
        x = jnp.concatenate([mixed[d, 0], mixed[d, 1]], axis=0)
        y = dot_pieces(halves(x), table)
        re = y[:ext, :LONG] - y[ext:, LONG:]
        im = y[ext:, :LONG] + y[:ext, LONG:]
        for i in range(share):
            for h in range(PARTS):
                start = (i * PARTS + h) * width
                outs[h][d * share + i, :, :width] = re[:, start : start + width]
                outs[h][d * share + i, :, width:] = im[:, start : start + width]


def middle_kernel(part, ext_in, spectrum, trig_hi, trig_lo, twist, ext_out, grid, mixed):
    count, ext, both = ext_in.shape
    width = both // 2
    rows = ext - RIM
    for s in range(count):
        grid[s * rows : (s + 1) * rows] = ext_in[s, :rows]
    upper = lax.broadcasted_iota(jnp.int32, (RIM, both), 0) < RIM // 2
    for s in range(count):
        rim = ext_in[s, rows:]
        after = (s + 1) % count * rows
        before = ((s + count - 1) % count + 1) * rows - RIM
        grid[after : after + RIM] = grid[after : after + RIM] + jnp.where(upper, rim, 0.0)
        grid[before : before + RIM] = grid[before : before + RIM] + jnp.where(upper, 0.0, rim)

    def forward(i, carry):
        start = pl.multiple_of(i * 8, 8)
        x = []
        for j in range(RADIX):
            strip = pl.ds(pl.multiple_of(j * LONG + start, 8), 8)
            x.append((grid[strip, :width], grid[strip, width:]))
        for e, (re, im) in enumerate(dft8(x, -1.0)):
            c = twist[pl.ds(start, 8), e : e + 1]
            s = twist[pl.ds(start, 8), RADIX + e : RADIX + e + 1]
            mixed[e, pl.ds(start, 8), :width] = re * c - im * s
            mixed[e, pl.ds(start, 8), width:] = re * s + im * c
        return carry

    lax.fori_loop(0, LONG // 8, forward, 0)
    table = (trig_hi[...], trig_lo[...])
    scale = 1.0 / (G * G)
    for e in range(RADIX):
        y = dot_pieces(table, halves(mixed[e]))
        factor = spectrum[e, :, part * width : (part + 1) * width] * scale
        re = (y[:LONG, :width] - y[LONG:, width:]) * factor
        im = (y[:LONG, width:] + y[LONG:, :width]) * factor
        y = dot_pieces(table, halves(jnp.concatenate([re, im], axis=1)))
        re = y[:LONG, :width] + y[LONG:, width:]
        im = y[:LONG, width:] - y[LONG:, :width]
        c = twist[:, e : e + 1]
        s = twist[:, RADIX + e : RADIX + e + 1]
        mixed[e, :, :width] = re * c + im * s
        mixed[e, :, width:] = im * c - re * s

    def backward(i, carry):
        start = pl.multiple_of(i * 8, 8)
        strip = pl.ds(start, 8)
        x = [(mixed[e, strip, :width], mixed[e, strip, width:]) for e in range(RADIX)]
        for j, (re, im) in enumerate(dft8(x, 1.0)):
            out = pl.ds(pl.multiple_of(j * LONG + start, 8), 8)
            grid[out, :width] = re
            grid[out, width:] = im
        return carry

    lax.fori_loop(0, LONG // 8, backward, 0)
    for s in range(count):
        ext_out[s, :rows] = grid[s * rows : (s + 1) * rows]
        after = (s + 1) % count * rows
        before = ((s + count - 1) % count + 1) * rows - RIM
        ext_out[s, rows:] = jnp.where(
            upper, grid[after : after + RIM], grid[before : before + RIM]
        )


def gather_kernel(rows, cols, frac, trig_hi, trig_lo, twist, *rest):
    ins, out, (field, mixed) = rest[:PARTS], rest[PARTS], rest[PARTS + 1 :]
    tiles, ext = field.shape[1], field.shape[2]
    count = ins[0].shape[0]
    width = ins[0].shape[2] // 2
    share = count // RADIX
    table = (trig_hi[...], trig_lo[...])
    for d in range(RADIX):
        blocks = [(d * share + i, h) for i in range(share) for h in range(PARTS)]
        re = jnp.concatenate([ins[h][b, :, :width] for b, h in blocks], axis=1)
        im = jnp.concatenate([ins[h][b, :, width:] for b, h in blocks], axis=1)
        y = dot_pieces(halves(jnp.concatenate([re, im], axis=0)), table)
        re = y[:ext, :LONG] + y[ext:, LONG:]
        im = y[ext:, :LONG] - y[:ext, LONG:]
        c = twist[d : d + 1, :]
        s = twist[RADIX + d : RADIX + d + 1, :]
        mixed[d, 0] = re * c + im * s
        mixed[d, 1] = im * c - re * s

    def one_strip(i, carry):
        strip = pl.ds(pl.multiple_of(i * 8, 8), 8)
        for h in range(LONG // TC):
            lanes = slice(h * TC, (h + 1) * TC)
            x = [(mixed[d, 0, strip, lanes], mixed[d, 1, strip, lanes]) for d in range(RADIX)]
            for j, (re, im) in enumerate(dft8(x, 1.0)):
                field[0, j * (LONG // TC) + h, strip, :] = re
                field[1, j * (LONG // TC) + h, strip, :] = im
        return carry

    lax.fori_loop(0, ext // 8, one_strip, 0)

    def one_tile(t, carry):
        row_tab = stencil_table(rows[pl.ds(t, 1), :], frac[0, pl.ds(t, 1), :], ext)
        col_tab = stencil_table(cols[pl.ds(t, 1), :], frac[1, pl.ds(t, 1), :], 2 * TC)
        after = lax.rem(t + 1, tiles)
        before = lax.rem(t + tiles - 1, tiles)
        low = lax.broadcasted_iota(jnp.int32, (ext, TC), 1) < TC // 2
        near = jnp.concatenate(
            [
                jnp.concatenate(
                    [field[k, t], jnp.where(low, field[k, after], field[k, before])], axis=1
                )
                for k in range(2)
            ],
            axis=0,
        )
        blended = dot_pieces(halves(near), halves(col_tab))
        for k in range(2):
            value = jnp.sum(row_tab * blended[k * ext : (k + 1) * ext], axis=0, keepdims=True)
            out[k, pl.ds(t, 1), :] = value
        return carry

    lax.fori_loop(0, tiles, one_tile, 0)


def split_table(table):
    high = table.astype(np.float32).astype(BF16)
    low = (table - high.astype(np.float64)).astype(np.float32).astype(BF16)
    return jnp.asarray(high), jnp.asarray(low)


def column_order(share, count, ranks, width):
    kept = width // (RADIX * share)
    order = [
        (width // RADIX) * (ranks * s + r) + i * kept + k
        for i in range(share)
        for r in range(ranks)
        for s in range(count)
        for k in range(kept)
    ]
    return np.array(order)


def exchanged_spectrum(spectrum, count, ranks):
    share = count // RADIX
    width = spectrum.shape[1]
    late = width % (RADIX * share) == 0
    if not late:
        spectrum = lax.all_gather(spectrum, "rhs", axis=1, tiled=True)
        width = spectrum.shape[1]
        ranks = 1
    kept = width // (RADIX * share)
    turned = spectrum.T.reshape(share, kept, RADIX, G).transpose(2, 0, 1, 3)
    turned = lax.all_to_all(turned.reshape(count, kept, G), "slab", 0, 0, tiled=True)
    turned = turned.reshape(count * kept, G)
    if late:
        turned = lax.all_gather(turned, "rhs", axis=0, tiled=True)
    by_residue = turned.T.reshape(LONG, RADIX, -1).transpose(1, 0, 2)
    return by_residue, column_order(share, count, ranks, width)


def total(partial):
    return jnp.sum(lax.all_gather(partial, "slab"), axis=0)


def per_device(targets, counts, cell_rows, cell_cols, fractions, spectrum, noise_var):
    tiles, capacity = cell_rows.shape
    count = lax.axis_size("slab")
    ranks = lax.axis_size("rhs")
    rows_dev = G // count
    ext = rows_dev + RIM
    width = G // count // PARTS
    both = 2 * width
    block = jax.ShapeDtypeStruct((count, ext, both), F32)

    factors, order = exchanged_spectrum(spectrum, count, ranks)
    short = np.arange(LONG)
    angle = (short[:, None] * order[None, :] % LONG) * (2.0 * np.pi / LONG)
    forth = split_table(np.concatenate([np.cos(angle), -np.sin(angle)], axis=1))
    back = split_table(np.concatenate([np.cos(angle).T, -np.sin(angle).T], axis=1))
    angle = (short[:, None] * short[None, :] % LONG) * (2.0 * np.pi / LONG)
    inner = split_table(np.concatenate([np.cos(angle), -np.sin(angle)], axis=0))
    angle = np.arange(RADIX)[:, None] * short[None, :] * (2.0 * np.pi / G)
    twist = np.concatenate([np.cos(angle), -np.sin(angle)], axis=0).astype(np.float32)
    twist_rows, twist_cols = jnp.asarray(twist.T), jnp.asarray(twist)
    scratch = [
        pltpu.VMEM((2, tiles, ext, TC), F32),
        pltpu.VMEM((RADIX, 2, ext, LONG), F32),
    ]

    slot_index = lax.broadcasted_iota(jnp.int32, (tiles, capacity), 1)
    live = (slot_index < counts[:, None]).astype(F32)

    def smoothed(direction):
        sent = pl.pallas_call(
            spread_kernel, out_shape=[block] * PARTS, scratch_shapes=scratch, name="spread"
        )(direction, cell_rows, cell_cols, fractions, *forth, twist_cols)
        returned = []
        for part in range(PARTS):
            there = lax.all_to_all(sent[part], "slab", 0, 0, tiled=True)
            weighed = pl.pallas_call(
                functools.partial(middle_kernel, part),
                out_shape=block,
                scratch_shapes=[
                    pltpu.VMEM((G, both), F32),
                    pltpu.VMEM((RADIX, LONG, both), F32),
                ],
                name="middle",
            )(there, factors, *inner, twist_rows)
            returned.append(lax.all_to_all(weighed, "slab", 0, 0, tiled=True))
        return pl.pallas_call(
            gather_kernel,
            out_shape=jax.ShapeDtypeStruct(direction.shape, F32),
            scratch_shapes=scratch,
            name="gather",
        )(cell_rows, cell_cols, fractions, *back, twist_cols, *returned)

    residual = live[None] * targets
    solution = jnp.zeros(residual.shape, F32)
    direction = residual
    norm_now = total(jnp.sum(residual * residual, axis=(1, 2)))
    for repeat in range(ITERS):
        image = live[None] * smoothed(direction) + noise_var[0] * direction
        product = total(jnp.sum(direction * image, axis=(1, 2)))
        alpha = (norm_now / product)[:, None, None]
        solution = solution + alpha * direction
        residual = residual - alpha * image
        if repeat + 1 < ITERS:
            norm_next = total(jnp.sum(residual * residual, axis=(1, 2)))
            direction = residual + (norm_next / norm_now)[:, None, None] * direction
            norm_now = norm_next
    return (solution, residual)


def solution(mesh):
    placed = (
        P("rhs", "slab", None),
        P("slab"),
        P("slab", None),
        P("slab", None),
        P(None, "slab", None),
        P(None, ("slab", "rhs")),
        P(),
    )
    return jax.shard_map(
        per_device,
        mesh=mesh,
        in_specs=placed,
        out_specs=(P("rhs", "slab", None), P("rhs", "slab", None)),
        check_vma=False,
    )
```

time: 1020 us -> 579 us (0.57)
  matrix products: 327 us -> 0 us
  local copies, waits for them, and re-layouts: 280 us -> 14.5 us
  blocking collectives: 60.3 us -> 213 us
  Pallas kernels: 0 us -> 111 us
  waiting for transfers between devices: 229 us -> 188 us
  other arithmetic: 43.2 us -> 7.79 us
  starting transfers between devices: 56.6 us -> 27.3 us
    dot_general x68 -> x0, matrix products: 327 us -> none  [the longest x32 146 us: contract_first(): jnp.einsum('kn,anmb->akmb', table, values, precision=lax.Precision.HIGHEST)]
    all_to_all x0 -> x3, blocking collectives: none -> 158 us  [the longest x2 104 us: smoothed(): there = lax.all_to_all(sent[part], 'slab', 0, 0, tiled=True)]
    pallas_call x0 -> x8, Pallas kernels: none -> 111 us  [the longest x4 46.3 us: smoothed(): pl.pallas_call(functools.partial(middle_kernel, part), out_shape=block, s...]
    psum x3 -> x0, blocking collectives: 60.3 us -> none  [the longest x2 38.5 us: squares(): return lax.psum(jnp.sum(residual * residual, axis=(1, 2)), 'slab')]
    all_to_all x8 -> x6, waiting for transfers between devices: 221 us -> 162 us  [the longest x3 123 us: smoothed(): returned.append(lax.all_to_all(weighed, 'slab', 0, 0, tiled=True))]
    unnamed x0 -> x3, blocking collectives: none -> 55.4 us
    slice x24 -> x0, local copies, waits for them, and re-layouts: 54 us -> none  [the longest x4 19.1 us: spread(): main_part = pieces[..., :TC].reshape(batch_rhs, ext_rows, tile_count * TC)]
    reshape x8 -> x2, local copies, waits for them, and re-layouts: 56.3 us -> 5.78 us  [the longest x1 3.64 us: exchanged_spectrum(): by_residue = turned.T.reshape(LONG, RADIX, -1).transpose(1, 0, 2)]
  transfers between devices with their start and end apart: 17 -> 7, of which waited for: 11 -> 6; matrix products, arithmetic and copies ran while one was open for 15% -> 2% of each run, Pallas kernels for 0% -> 11%
where the time goes in v1:
time: 579 us; the launch traced here: 578 us
  blocking collectives  213 us (37%)
  waiting for transfers between devices  188 us (32%)
  Pallas kernels  111 us (19%)
  starting transfers between devices  27.3 us (5%)
  between operations  15.4 us (3%)
  local copies, waits for them, and re-layouts  14.5 us (3%)
  other arithmetic  7.79 us (1%)
    all_to_all x3, waiting for transfers between devices, smoothed(): returned.append(lax.all_to_all(weighed, 'slab', 0, 0, tiled=True))  123 us
    all_to_all x2, blocking collectives, smoothed(): there = lax.all_to_all(sent[part], 'slab', 0, 0, tiled=True)  104 us
    unnamed x3, blocking collectives  55.4 us
    all_to_all x1, blocking collectives, smoothed(): returned.append(lax.all_to_all(weighed, 'slab', 0, 0, tiled=True))  54.2 us
    pallas_call x4, Pallas kernels, smoothed(): pl.pallas_call(functools.partial(middle_kernel, part), out_shape=block, s...  46.3 us
    all_to_all x2, waiting for transfers between devices, smoothed(): there = lax.all_to_all(sent[part], 'slab', 0, 0, tiled=True)  38.6 us
    pallas_call x2, Pallas kernels, smoothed(): pl.pallas_call(spread_kernel, out_shape=[block] * PARTS, scratch_shapes=s...  34.1 us
    pallas_call x2, Pallas kernels, smoothed(): pl.pallas_call(gather_kernel, out_shape=jax.ShapeDtypeStruct(direction.sh...  31 us
  transfers between devices with their start and end apart: 7, of which 6 were waited for; matrix products, arithmetic and copies ran while one was open for 2% of the time, Pallas kernels for 11%

profile of v1, /device:TPU:0, one launch (start us, length us, event | category | flops | bytes accessed | tf_op | source)
XLA Modules:
  0.0 577.6 jit_solution(2575393855368924846)
XLA Ops:
  9.3 7.3 %all-to-all-start.1 = ((f32[8,8,2048]{2,1,0:T(8,128)}), f32[8,8,2048]{2,1,0:T(8,128)S(1)}, u32[]{:S(2)}, u32[]{:S(2)}) async-start(f32[8,8,2048]{2,1,0:T(8,128)} %copy.22), calls=%async_computation.1 | async-start | bytes 1048576 | tf_op jit(solution)/shard_map/all_to_all | solution.py:287
  18.7 17.1 %spread.2 = (f32[8,264,256]{2,1,0:T(8,128)}, f32[8,264,256]{2,1,0:T(8,128)}) custom-call(f32[2,16,256]{2,1,0:T(8,128)} %broadcast_multiply_fusion.vec, s32[16,256]{1,0:T(8,128)} %rows.7, s32[16,256]{1,0:T(8,128)} %cols.7, f32[2,16,256]{2,1,0:T(8,128)} %frac.7, bf16[256,512]{1,0:T(8,128)(2,1)} %constant.18.clone.trig_hi, ...), custom_call_target="tpu_custom_call" | custom-call | tf_op jit(solution)/shard_map/spread/pallas_call | solution.py:328
  35.8 55.9 %all_to_all.45.ext_in = f32[8,264,256]{2,1,0:T(8,128)} all-to-all(f32[8,264,256]{2,1,0:T(8,128)} %get-tuple-element.6), channel_id=1, replica_groups=mesh['slab'=8,'rhs'=4] {'slab'}, dimensions={0} | all-to-all | bytes 4325376 | tf_op jit(solution)/shard_map/all_to_all | solution.py:333
  96.0 25.6 %all-gather.6.cloned.1.call-done = f32[256,2048]{1,0:T(8,128)} async-done(((f32[64,2048]{1,0:T(8,128)}), f32[256,2048]{1,0:T(8,128)}) %all-gather.6.cloned.1.call-update) | async-done | bytes 2097168 | tf_op jit(solution)/shard_map/all_gather | solution.py:290
  128.2 11.6 %middle.4 = f32[8,264,256]{2,1,0:T(8,128)} custom-call(f32[8,264,256]{2,1,0:T(8,128)} %all_to_all.45.ext_in, f32[8,256,256]{2,1,0:T(8,128)} %bitcast.20, bf16[512,256]{1,0:T(8,128)(2,1)} %constant.22.clone.trig_hi, bf16[512,256]{1,0:T(8,128)(2,1)} %constant.23.clone.trig_lo, f32[256,16]{1,0:T(8,128)} %constant.24.clone.twist), custom_call_target="tpu_custom_call" | custom-call | tf_op jit(solution)/shard_map/middle/pallas_call | solution.py:334
  139.7 4.1 all-to-all-done.3.ext_in
  149.0 11.6 %middle.5 = f32[8,264,256]{2,1,0:T(8,128)} custom-call(f32[8,264,256]{2,1,0:T(8,128)} %copy-done.1, f32[8,256,256]{2,1,0:T(8,128)} %bitcast.21, bf16[512,256]{1,0:T(8,128)(2,1)} %constant.22.clone.trig_hi, bf16[512,256]{1,0:T(8,128)(2,1)} %constant.23.clone.trig_lo, f32[256,16]{1,0:T(8,128)} %constant.24.clone.twist), custom_call_target="tpu_custom_call" | custom-call | tf_op jit(solution)/shard_map/middle/pallas_call | solution.py:334
  160.5 38.1 %all-to-all-done.2.rest_0_ = f32[8,264,256]{2,1,0:T(8,128)S(1)} async-done(((f32[8,264,256]{2,1,0:T(8,128)}), f32[8,264,256]{2,1,0:T(8,128)S(1)}, u32[]{:S(2)}, u32[]{:S(2)}) %all-to-all-start.2) | async-done | bytes 2162720 | tf_op jit(solution)/shard_map/all_to_all | solution.py:343
  200.0 4.4 all-to-all-start.4
  206.3 47.2 %all-to-all-done.4.rest_1_ = f32[8,264,256]{2,1,0:T(8,128)} async-done(((f32[8,264,256]{2,1,0:T(8,128)}), f32[8,264,256]{2,1,0:T(8,128)}, u32[]{:S(2)}, u32[]{:S(2)}) %all-to-all-start.4) | async-done | bytes 2162720 | tf_op jit(solution)/shard_map/all_to_all | solution.py:343
  253.5 15.5 %gather.2 = f32[2,16,256]{2,1,0:T(8,128)} custom-call(s32[16,256]{1,0:T(8,128)} %rows.7, s32[16,256]{1,0:T(8,128)} %cols.7, f32[2,16,256]{2,1,0:T(8,128)} %frac.7, bf16[256,512]{1,0:T(8,128)(2,1)} %constant.20.clone.trig_hi, bf16[256,512]{1,0:T(8,128)(2,1)} %constant.21.clone.trig_lo, f32[16,256]{1,0:T(8,128)} %constant.25.clone.twist, ...), custom_call_target="tpu_custom_call" | custom-call | tf_op jit(solution)/shard_map/gather/pallas_call | solution.py:344
  270.4 19.5 %all-reduce.4 = (f32[16]{0:T(128)S(1)}, f32[16]{0:T(128)S(1)}) all-reduce(f32[16]{0:T(128)S(1)} %dynamic-update-slice, f32[16]{0:T(128)S(1)} %dynamic-update-slice.1), channel_id=2, replica_groups=mesh['slab'=8,'rhs'=4] {'slab'}, use_global_device_ids=true, to_apply=%add | all-reduce | flops 32 | bytes 256
  291.2 17.1 %all-reduce.2 = f32[16]{0:T(128)S(1)} all-reduce(f32[16]{0:T(128)S(1)} %dynamic-update-slice.2), channel_id=4, replica_groups=mesh['slab'=8,'rhs'=4] {'slab'}, use_global_device_ids=true, to_apply=%add.2 | all-reduce | flops 16 | bytes 128
  309.8 17.1 %spread.3 = (f32[8,264,256]{2,1,0:T(8,128)}, f32[8,264,256]{2,1,0:T(8,128)}) custom-call(f32[2,16,256]{2,1,0:T(8,128)} %multiply_add_fusion.2.vec, s32[16,256]{1,0:T(8,128)} %rows.7, s32[16,256]{1,0:T(8,128)} %cols.7, f32[2,16,256]{2,1,0:T(8,128)} %frac.7, bf16[256,512]{1,0:T(8,128)(2,1)} %constant.18.clone.trig_hi, ...), custom_call_target="tpu_custom_call" | custom-call | tf_op jit(solution)/shard_map/spread/pallas_call | solution.py:328
  326.9 47.9 %all_to_all.46.ext_in = f32[8,264,256]{2,1,0:T(8,128)} all-to-all(f32[8,264,256]{2,1,0:T(8,128)} %get-tuple-element.9), channel_id=1, replica_groups=mesh['slab'=8,'rhs'=4] {'slab'}, dimensions={0} | all-to-all | bytes 4325376 | tf_op jit(solution)/shard_map/all_to_all | solution.py:333
  374.8 3.8 all-to-all-start.5
  378.7 11.6 %middle.7 = f32[8,264,256]{2,1,0:T(8,128)} custom-call(f32[8,264,256]{2,1,0:T(8,128)} %all_to_all.46.ext_in, f32[8,256,256]{2,1,0:T(8,128)} %bitcast.22, bf16[512,256]{1,0:T(8,128)(2,1)} %constant.22.clone.trig_hi, bf16[512,256]{1,0:T(8,128)(2,1)} %constant.23.clone.trig_lo, f32[256,16]{1,0:T(8,128)} %constant.24.clone.twist), custom_call_target="tpu_custom_call" | custom-call | tf_op jit(solution)/shard_map/middle/pallas_call | solution.py:334
  390.2 34.5 %all-to-all-done.5.ext_in = f32[8,264,256]{2,1,0:T(8,128)S(1)} async-done(((f32[8,264,256]{2,1,0:T(8,128)}), f32[8,264,256]{2,1,0:T(8,128)S(1)}, u32[]{:S(2)}, u32[]{:S(2)}) %all-to-all-start.5) | async-done | bytes 2162720 | tf_op jit(solution)/shard_map/all_to_all | solution.py:333
  426.1 4.4 all-to-all-start.8
  430.4 11.6 %middle.6 = f32[8,264,256]{2,1,0:T(8,128)} custom-call(f32[8,264,256]{2,1,0:T(8,128)} %copy-done.2, f32[8,256,256]{2,1,0:T(8,128)} %bitcast.23, bf16[512,256]{1,0:T(8,128)(2,1)} %constant.22.clone.trig_hi, bf16[512,256]{1,0:T(8,128)(2,1)} %constant.23.clone.trig_lo, f32[256,16]{1,0:T(8,128)} %constant.24.clone.twist), custom_call_target="tpu_custom_call" | custom-call | tf_op jit(solution)/shard_map/middle/pallas_call | solution.py:334
  442.0 37.6 %all-to-all-done.8.rest_1_ = f32[8,264,256]{2,1,0:T(8,128)} async-done(((f32[8,264,256]{2,1,0:T(8,128)}), f32[8,264,256]{2,1,0:T(8,128)}, u32[]{:S(2)}, u32[]{:S(2)}) %all-to-all-start.8) | async-done | bytes 2162720 | tf_op jit(solution)/shard_map/all_to_all | solution.py:343
  479.6 54.2 %all_to_all.47.rest_0_ = f32[8,264,256]{2,1,0:T(8,128)} all-to-all(f32[8,264,256]{2,1,0:T(8,128)} %middle.6), channel_id=1, replica_groups=mesh['slab'=8,'rhs'=4] {'slab'}, dimensions={0} | all-to-all | bytes 4325376 | tf_op jit(solution)/shard_map/all_to_all | solution.py:343
  533.8 15.5 %gather.3 = f32[2,16,256]{2,1,0:T(8,128)} custom-call(s32[16,256]{1,0:T(8,128)} %rows.7, s32[16,256]{1,0:T(8,128)} %cols.7, f32[2,16,256]{2,1,0:T(8,128)} %frac.7, bf16[256,512]{1,0:T(8,128)(2,1)} %constant.20.clone.trig_hi, bf16[256,512]{1,0:T(8,128)(2,1)} %constant.21.clone.trig_lo, f32[16,256]{1,0:T(8,128)} %constant.25.clone.twist, ...), custom_call_target="tpu_custom_call" | custom-call | tf_op jit(solution)/shard_map/gather/pallas_call | solution.py:344
  550.4 18.8 %all-reduce.3 = f32[16]{0:T(128)S(1)} all-reduce(f32[16]{0:T(128)S(1)} %dynamic-update-slice.3), channel_id=5, replica_groups=mesh['slab'=8,'rhs'=4] {'slab'}, use_global_device_ids=true, to_apply=%add.3 | all-reduce | flops 16 | bytes 128
  (51 shorter events, 30.4 us)
Async XLA Ops:
  9.3 26.5 %all-to-all-start.1 = ((f32[8,8,2048]{2,1,0:T(8,128)}), f32[8,8,2048]{2,1,0:T(8,128)S(1)}, u32[]{:S(2)}, u32[]{:S(2)}) async-start(f32[8,8,2048]{2,1,0:T(8,128)} %copy.22), calls=%async_computation.1 | async-start | bytes 1048576 | tf_op jit(solution)/shard_map/all_to_all | solution.py:287
  35.8 55.9 %copy-start.3 = (f32[8,8,2048]{2,1,0:T(8,128)}, f32[8,8,2048]{2,1,0:T(8,128)S(1)}, u32[]{:S(2)}) copy-start(f32[8,8,2048]{2,1,0:T(8,128)S(1)} %all-to-all-done.1) | copy-start | bytes 1572868
  91.7 52.2 %all-to-all-start.3 = ((f32[8,264,256]{2,1,0:T(8,128)}), f32[8,264,256]{2,1,0:T(8,128)S(1)}, u32[]{:S(2)}, u32[]{:S(2)}) async-start(f32[8,264,256]{2,1,0:T(8,128)} %get-tuple-element.7), calls=%async_computation.3 | async-start | bytes 4325376 | tf_op jit(solution)/shard_map/all_to_all | solution.py:333
  95.3 26.3 %all-gather.6.cloned.1.call-start = ((), (), s32[]{:S(2)}) async-start(), calls=%async_computation.9 | async-start | bytes 2621440 | tf_op jit(solution)/shard_map/all_gather | solution.py:290
  143.8 1.3 copy-start.1
  145.2 53.5 %all-to-all-start.2 = ((f32[8,264,256]{2,1,0:T(8,128)}), f32[8,264,256]{2,1,0:T(8,128)S(1)}, u32[]{:S(2)}, u32[]{:S(2)}) async-start(f32[8,264,256]{2,1,0:T(8,128)} %middle.4), calls=%async_computation.2 | async-start | bytes 4325376 | tf_op jit(solution)/shard_map/all_to_all | solution.py:343
  160.5 44.5 %copy-start.7 = (u32[32]{0:T(128)S(1)}, u32[32]{0:T(128)}, u32[]{:S(2)}) copy-start(u32[32]{0:T(128)} %constant.29) | copy-start | bytes 388
  198.7 1.3 copy-start
  200.0 53.5 %all-to-all-start.4 = ((f32[8,264,256]{2,1,0:T(8,128)}), f32[8,264,256]{2,1,0:T(8,128)}, u32[]{:S(2)}, u32[]{:S(2)}) async-start(f32[8,264,256]{2,1,0:T(8,128)} %middle.5), calls=%async_computation.4 | async-start | bytes 4325376 | tf_op jit(solution)/shard_map/all_to_all | solution.py:343
  206.3 62.7 %copy-start.5 = (f32[2,16,256]{2,1,0:T(8,128)S(1)}, f32[2,16,256]{2,1,0:T(8,128)}, u32[]{:S(2)}) copy-start(f32[2,16,256]{2,1,0:T(8,128)} %param.15) | copy-start | bytes 98308
  374.8 49.9 %all-to-all-start.5 = ((f32[8,264,256]{2,1,0:T(8,128)}), f32[8,264,256]{2,1,0:T(8,128)S(1)}, u32[]{:S(2)}, u32[]{:S(2)}) async-start(f32[8,264,256]{2,1,0:T(8,128)} %get-tuple-element.8), calls=%async_computation.5 | async-start | bytes 4325376 | tf_op jit(solution)/shard_map/all_to_all | solution.py:333
  424.7 1.4 copy-start.2
  426.1 53.6 %all-to-all-start.8 = ((f32[8,264,256]{2,1,0:T(8,128)}), f32[8,264,256]{2,1,0:T(8,128)}, u32[]{:S(2)}, u32[]{:S(2)}) async-start(f32[8,264,256]{2,1,0:T(8,128)} %middle.7), calls=%async_computation.8 | async-start | bytes 4325376 | tf_op jit(solution)/shard_map/all_to_all | solution.py:343
  533.8 15.5 %copy-start.6 = (f32[2,16,256]{2,1,0:T(8,128)S(1)}, f32[2,16,256]{2,1,0:T(8,128)}, u32[]{:S(2)}) copy-start(f32[2,16,256]{2,1,0:T(8,128)} %multiply_add_fusion.2.vec) | copy-start | bytes 98308
  533.8 35.5 %copy-start.4 = (f32[2,16,256]{2,1,0:T(8,128)S(1)}, f32[2,16,256]{2,1,0:T(8,128)}, u32[]{:S(2)}) copy-start(f32[2,16,256]{2,1,0:T(8,128)} %gather.2) | copy-start | bytes 98308
Sparse Core Ops, SparseCore 0:
  97.6 23.9 all-gather.5
